TPU v7x, 256 devices: a whole 4x4x8 slice. The times are simulated.
256 devices in a mesh: dof: 16 (over x, y_hi, core), tm: 16 (over z, y_lo).
Axes of the slice: x: 4, y: 4 (y_hi: 2, y_lo: 2; y = y_hi * 2 + y_lo), z: 8, core: 2. Of those that a mesh axis runs over, the one named last changes fastest.
Arguments:
- snapshots: bfloat16 [327680, 4096], P('dof', 'tm'), may hold values from -6 to 6
- basis: bfloat16 [327680, 64], P('dof'), may hold values from -0.009765625 to 0.009765625
Outputs:
- gram: float32 [2144, 2144], P('tm', 'dof')
- coords: float32 [64, 4096], P(None, 'tm')
All inputs are finite; a program needn't handle non-finite values.
Results may differ from a plain program's by a relative error of at most 0.0021.
Values may be sent and summed in bfloat16 or wider, within the bound.
A program may use at most 64 MiB of HBM per device.

v0:
```python
import jax
import jax.numpy as jnp
import numpy as np
from jax import lax
from jax.sharding import PartitionSpec as P


def sent_to_all(shard, axis):
    copies = jnp.broadcast_to(shard, (lax.axis_size(axis), *shard.shape))
    return lax.all_to_all(copies, axis, split_axis=0, concat_axis=0, tiled=True)


def over_copies(shard, axis):
    return sent_to_all(shard, axis).sum(axis=0)


def cut_along(shard, dim, size):
    before, after = (shard.shape[:dim], shard.shape[dim + 1 :])
    return jnp.moveaxis(shard.reshape(*before, size, -1, *after), dim, 0)


def summed_on_arrival(shard, axis, dim):
    parts = cut_along(shard, dim, lax.axis_size(axis))
    arrived = lax.all_to_all(parts, axis, split_axis=0, concat_axis=0, tiled=True)
    return arrived.astype(jnp.float32).sum(axis=0)


def build_features(coords):
    modes = coords.shape[0]
    upper_i, upper_j = np.triu_indices(modes)
    quad = coords[upper_i, :] * coords[upper_j, :]
    return jnp.concatenate([coords, quad], axis=0).astype(jnp.bfloat16)


def on_device(snapshots, basis):
    partial_proj = lax.dot_general(
        basis, snapshots, (((0,), (0,)), ((), ())), preferred_element_type=jnp.float32
    )
    coords = over_copies(partial_proj, "dof")
    features = build_features(coords)
    feature_count = features.shape[0]
    inverse_total = 1.0 / (features.shape[1] * lax.axis_size("tm"))
    owned_rows = feature_count // lax.axis_size("tm")
    col_width = feature_count // lax.axis_size("dof")
    col_start = lax.axis_index("dof") * col_width
    column_block = lax.dynamic_slice_in_dim(features, col_start, col_width, 0)
    block = lax.slice_in_dim(features, 0, owned_rows * lax.axis_size("tm"), axis=0)
    product = lax.dot_general(
        block, column_block, (((1,), (1,)), ((), ())), preferred_element_type=jnp.float32
    )
    gram = summed_on_arrival((product * inverse_total).astype(jnp.bfloat16), "tm", 0)
    return (gram, coords)


def solution(mesh):
    placed = (P("dof", "tm"), P("dof", None))
    return jax.shard_map(
        on_device,
        mesh=mesh,
        in_specs=placed,
        out_specs=(P("tm", "dof"), P(None, "tm")),
        check_vma=False,
    )
```

profile of v0, /device:TPU:1, one launch (start us, length us, event | category | flops | bytes accessed | tf_op | source)
XLA Modules:
  0.0 100.6 jit_solution(9762633188567180609)
XLA Ops:
  0.6 0.0 copy-start
  0.6 1.7 %copy-done = bf16[20480,64]{0,1:T(8,128)(2,1)S(1)} copy-done((bf16[20480,64]{0,1:T(8,128)(2,1)S(1)}, bf16[20480,64]{0,1:T(8,128)(2,1)}, u32[]{:S(2)}) %copy-start) | copy-done | bytes 2621464
  2.4 5.8 %fusion.6 = f32[64,256]{1,0:T(8,128)S(1)} fusion(bf16[20480,64]{0,1:T(8,128)(2,1)S(1)} %copy-done, bf16[20480,256]{1,0:T(8,128)(2,1)} %param.6), kind=kOutput, calls=%fused_computation.15 | convolution fusion | flops 671088640 | bytes 13172736 | tf_op jit(solution)/shard_map/dot_general | solution.py:36
  8.2 0.0 copy-start.3
  8.2 0.0 copy-start.2
  8.2 1.1 %broadcast_in_dim.9 = f32[16,64,256]{2,1,0:T(8,128)} broadcast(f32[64,256]{1,0:T(8,128)S(1)} %fusion.6), dimensions={1,2} | broadcast | bytes 1114112 | tf_op jit(solution)/shard_map/broadcast_in_dim | solution.py:9
  9.3 8.4 %all-to-all-start = ((f32[16,64,256]{2,1,0:T(8,128)}), f32[16,64,256]{2,1,0:T(8,128)}, u32[]{:S(2)}, u32[]{:S(2)}) async-start(f32[16,64,256]{2,1,0:T(8,128)} %broadcast_in_dim.9), calls=%async_computation | async-start | bytes 2097152 | tf_op jit(solution)/shard_map/all_to_all | solution.py:10
  17.8 0.0 copy-done.3
  17.8 0.0 copy-done.2
  17.8 17.0 %all-to-all-done = f32[16,64,256]{2,1,0:T(8,128)} async-done(((f32[16,64,256]{2,1,0:T(8,128)}), f32[16,64,256]{2,1,0:T(8,128)}, u32[]{:S(2)}, u32[]{:S(2)}) %all-to-all-start) | async-done | bytes 1048608 | tf_op jit(solution)/shard_map/all_to_all | solution.py:10
  34.8 1.3 %reduce_sum.18 = f32[64,256]{1,0:T(8,128)S(1)} reduce(f32[16,64,256]{2,1,0:T(8,128)} %all-to-all-done, f32[]{:T(128)} %constant.5.clone.1), dimensions={0}, to_apply=%region_0.0 | reduce | flops 245760 | bytes 1114116 | tf_op jit(solution)/shard_map/reduce_sum | solution.py:14
  36.1 0.0 copy-start.1
  36.1 6.4 %gather_fusion = f32[2080,256]{1,0:T(8,128)} fusion(f32[64,256]{1,0:T(8,128)S(1)} %reduce_sum.18, s32[3072]{0:T(1024)S(1)} %pad_clamp_fusion.1), kind=kCustom, calls=%fused_computation | custom fusion | bytes 4268160 | tf_op jit(solution)/shard_map/gather | solution.py:31
  42.5 0.0 copy-done.1
  42.5 6.4 %gather_fusion.1 = f32[2080,256]{1,0:T(8,128)} fusion(f32[64,256]{1,0:T(8,128)S(1)} %reduce_sum.18, s32[3072]{0:T(1024)S(1)} %pad_clamp_fusion), kind=kCustom, calls=%fused_computation.1 | custom fusion | bytes 4268160 | tf_op jit(solution)/shard_map/gather | solution.py:31
  48.9 2.5 %multiply_convert_fusion = bf16[2080,256]{1,0:T(8,128)(2,1)S(1)} fusion(f32[2080,256]{1,0:T(8,128)} %gather_fusion, f32[2080,256]{1,0:T(8,128)} %gather_fusion.1), kind=kLoop, calls=%fused_computation.5 | loop fusion | flops 1064960 | bytes 5324800 | tf_op jit(solution)/shard_map/convert.1
  51.4 0.5 fusion
  51.9 3.9 %reshape.7 = bf16[16,134,134]{1,0,2:T(8,128)(2,1)} reshape(bf16[2144,134]{0,1:T(8,128)(2,1)S(1)} %fusion) | data formatting | bytes 1149184 | tf_op jit(solution)/shard_map/reshape | solution.py:19
  55.8 1.6 %copy.14 = bf16[16,134,134]{1,2,0:T(8,128)(2,1)S(1)} copy(bf16[16,134,134]{1,0,2:T(8,128)(2,1)} %reshape.7) | data formatting | bytes 1149184 | tf_op jit(solution)/shard_map/reshape | solution.py:19
  57.4 37.9 %all_to_all.10 = bf16[16,134,134]{1,2,0:T(8,128)(2,1)} all-to-all(bf16[16,134,134]{1,2,0:T(8,128)(2,1)S(1)} %copy.14), channel_id=1, replica_groups=mesh['dof'=16,'tm'=16] {'tm'}, dimensions={0} | all-to-all | bytes 1149184 | tf_op jit(solution)/shard_map/all_to_all | solution.py:24
  95.3 2.9 %copy.15 = bf16[16,134,134]{2,0,1:T(8,128)(2,1)} copy(bf16[16,134,134]{1,2,0:T(8,128)(2,1)} %all_to_all.10) | data formatting | bytes 1149184 | tf_op jit(solution)/shard_map/all_to_all | solution.py:24
  98.2 2.4 %convert_reduce_fusion = f32[134,134]{1,0:T(8,128)} fusion(bf16[16,134,134]{2,0,1:T(8,128)(2,1)} %copy.15), kind=kLoop, calls=%fused_computation.4 | loop fusion | flops 556636 | bytes 646416 | tf_op jit(solution)/shard_map/reduce_sum | solution.py:25
  (3 shorter events, 0.0 us)
Async XLA Ops:
  0.6 1.7 %copy-start = (bf16[20480,64]{0,1:T(8,128)(2,1)S(1)}, bf16[20480,64]{0,1:T(8,128)(2,1)}, u32[]{:S(2)}) copy-start(bf16[20480,64]{0,1:T(8,128)(2,1)} %param.7) | copy-start | bytes 7864324
  8.2 9.6 %copy-start.3 = (s32[2080]{0:T(1024)S(1)}, s32[2080]{0:T(1024)}, u32[]{:S(2)}) copy-start(s32[2080]{0:T(1024)} %constant.28) | copy-start | bytes 24964
  8.2 9.6 %copy-start.2 = (s32[2080]{0:T(1024)S(1)}, s32[2080]{0:T(1024)}, u32[]{:S(2)}) copy-start(s32[2080]{0:T(1024)} %constant.29) | copy-start | bytes 24964
  9.3 25.5 %all-to-all-start = ((f32[16,64,256]{2,1,0:T(8,128)}), f32[16,64,256]{2,1,0:T(8,128)}, u32[]{:S(2)}, u32[]{:S(2)}) async-start(f32[16,64,256]{2,1,0:T(8,128)} %broadcast_in_dim.9), calls=%async_computation | async-start | bytes 2097152 | tf_op jit(solution)/shard_map/all_to_all | solution.py:10
  36.1 6.4 %copy-start.1 = (f32[64,256]{1,0:T(8,128)}, f32[64,256]{1,0:T(8,128)S(1)}, u32[]{:S(2)}) copy-start(f32[64,256]{1,0:T(8,128)S(1)} %reduce_sum.18) | copy-start | bytes 196612
where the time goes:
time: 101 us
  blocking collectives  37.9 us (38%)
  local copies, waits for them, and re-layouts  24 us (24%)
  waiting for transfers between devices  17 us (17%)
  starting transfers between devices  8.43 us (8%)
  matrix products  6.3 us (6%)
  other arithmetic  6.2 us (6%)
    all_to_all x1, blocking collectives, summed_on_arrival(): lax.all_to_all(parts, axis, split_axis=0, concat_axis=0, tiled=True)  37.9 us
    all_to_all x1, waiting for transfers between devices, sent_to_all(): return lax.all_to_all(copies, axis, split_axis=0, concat_axis=0, tiled=True)  17 us
    gather x2, local copies, waits for them, and re-layouts, build_features(): quad = coords[upper_i, :] * coords[upper_j, :]  12.8 us
    all_to_all x1, starting transfers between devices, sent_to_all(): return lax.all_to_all(copies, axis, split_axis=0, concat_axis=0, tiled=True)  8.43 us
    dot_general x1, matrix products, on_device(): lax.dot_general(basis, snapshots, (((0,), (0,)), ((), ())), preferred_ele...  5.79 us
    reshape x2, local copies, waits for them, and re-layouts, cut_along(): return jnp.moveaxis(shard.reshape(*before, size, -1, *after), dim, 0)  5.5 us
    all_to_all x1, local copies, waits for them, and re-layouts, summed_on_arrival(): lax.all_to_all(parts, axis, split_axis=0, concat_axis=0, tiled=True)  2.88 us
    another operation x2, other arithmetic  2.46 us
  transfers between devices with their start and end apart: 1, of which 1 were waited for; matrix products, arithmetic and copies ran while one was open for 0% of the time, Pallas kernels for 0%

commit v1 on v0

v1 whole, which is shorter than its diff:
```python
import functools

import jax
import jax.numpy as jnp
from jax import lax
from jax.experimental import pallas as pl
from jax.experimental.pallas import tpu as pltpu
from jax.sharding import PartitionSpec as P

MESH = pl.DeviceIdType.MESH
R = 64
NT = 4096
W = 134
PAD = 144
CHUNKS = 20


def one_hot_pair(block):
    shape = (PAD, 256)
    feature = block * W + lax.broadcasted_iota(jnp.int32, shape, 0)
    lane = lax.broadcasted_iota(jnp.int32, shape, 1)
    mode = lane & (R - 1)
    data = lane < 3 * R
    pair = feature - R
    linear = feature < R
    start = mode * R - ((mode * (mode - 1)) >> 1)
    first = (start <= pair) & (pair < start + R - mode)
    shift = jnp.where(first & (lane < R), (mode - start).astype(jnp.float32), 0.0)
    second = pair.astype(jnp.float32) + jnp.sum(shift, axis=1, keepdims=True)
    def num(mask):
        return jnp.where(mask, jnp.float32(1), jnp.float32(0))

    hot_i = jnp.where(linear, num(mode == feature), num(first)) * num(data)
    hot_j = jnp.where(
        linear, num(lane == 3 * R), num(mode.astype(jnp.float32) == second) * num(data)
    )
    return hot_i.astype(jnp.bfloat16), hot_j.astype(jnp.bfloat16)


def kernel(
    basis_hbm, snap_hbm, gram_ref, coords_ref,
    basis, snap, hot_i, hot_j, part, got, tiles, gram_acc, gram_in, other_half,
    load_sem, rs_send, rs_recv, z_send, z_recv, p_send, p_recv, c_send, c_recv, g_send, g_recv,
):
    d = lax.axis_index("dof")
    t = lax.axis_index("tm")
    core = lax.rem(d, 2)
    group = d // 2
    x = d // 4
    y_hi = lax.rem(group, 2)
    z = t // 2
    y_lo = lax.rem(t, 2)
    chip = x * 4 + y_hi * 2 + y_lo
    partner = d + 1 - 2 * core
    depth = basis.shape[1] // CHUNKS

    def load(i):
        at = pl.ds(pl.multiple_of(i * depth, depth), depth)
        return (
            pltpu.make_async_copy(basis_hbm.at[:, at], basis.at[:, at], load_sem.at[0, i]),
            pltpu.make_async_copy(snap_hbm.at[at], snap.at[at], load_sem.at[1, i]),
        )

    def start_load(i, _):
        for copy in load(i):
            copy.start()
        return 0

    lax.fori_loop(0, CHUNKS, start_load, 0)

    barrier = pltpu.get_barrier_semaphore()

    def greet_dof(k, _):
        pl.semaphore_signal(
            barrier, inc=1, device_id={"dof": lax.rem(d + k, 16), "tm": t}, device_id_type=MESH
        )
        return 0

    def greet_z(k, _):
        to = lax.rem(z + k, 8) * 2 + y_lo
        pl.semaphore_signal(barrier, inc=1, device_id={"dof": d, "tm": to}, device_id_type=MESH)
        return 0

    def greet_plane(k, _):
        pl.semaphore_signal(
            barrier, inc=1,
            device_id={"dof": k * 2 + core, "tm": z * 2 + 1 - y_lo}, device_id_type=MESH,
        )
        return 0

    lax.fori_loop(1, 16, greet_dof, 0)
    lax.fori_loop(1, 8, greet_z, 0)
    lax.fori_loop(0, 8, greet_plane, 0)

    for n, block in enumerate((t, d, partner)):
        first, second = one_hot_pair(block)
        hot_i[pl.ds(n * PAD, PAD)] = first
        hot_j[pl.ds(n * PAD, PAD)] = second
    gram_acc[...] = jnp.zeros_like(gram_acc)

    def project(i, acc):
        for copy in load(i):
            copy.wait()
        at = pl.ds(pl.multiple_of(i * depth, depth), depth)
        return acc + jnp.dot(basis[:, at], snap[at], preferred_element_type=jnp.float32)

    acc = lax.fori_loop(0, CHUNKS, project, jnp.zeros((R, 256), jnp.float32))
    for g in range(8):
        for h in range(2):
            part[2 * g + h] = acc[8 * g : 8 * g + 8, 128 * h : 128 * h + 128]

    pl.semaphore_wait(barrier, 30)

    def rs_copy(k):
        to = lax.rem(d + k, 16)
        return pltpu.make_async_remote_copy(
            src_ref=part.at[to], dst_ref=got.at[d], send_sem=rs_send, recv_sem=rs_recv,
            device_id={"dof": to, "tm": t}, device_id_type=MESH,
        )

    def rs_start(k, _):
        rs_copy(k).start()
        return 0

    lax.fori_loop(1, 16, rs_start, 0)
    got[d] = part[d]

    def wait_tiles(n, sem):
        fifteen = tiles.at[0, pl.ds(0, n)]
        pltpu.make_async_copy(fifteen, fifteen, sem).wait()

    wait_tiles(15, rs_recv)
    mine = y_lo * 8 + group
    tiles[z, mine] = jnp.sum(got[...], axis=0)

    def z_copy(k):
        to = lax.rem(z + k, 8)
        return pltpu.make_async_remote_copy(
            src_ref=tiles.at[z, mine], dst_ref=tiles.at[z, mine],
            send_sem=z_send.at[to], recv_sem=z_recv.at[z],
            device_id={"dof": d, "tm": to * 2 + y_lo}, device_id_type=MESH,
        )

    def z_start(k, _):
        z_copy(k).start()
        return 0

    lax.fori_loop(1, 8, z_start, 0)

    def order(s):
        return lax.rem(z + 8 + ((s + 1) // 2) * (2 * lax.rem(s, 2) - 1), 8)

    def p_start_at(slot):
        def start(k, _):
            to = lax.rem(chip + k, 16)
            to_x, to_hi, to_lo = to // 4, lax.rem(to // 2, 2), lax.rem(to, 2)
            pltpu.make_async_remote_copy(
                src_ref=tiles.at[slot, mine], dst_ref=tiles.at[slot, mine],
                send_sem=p_send.at[slot], recv_sem=p_recv.at[slot],
                device_id={"dof": (to_x * 2 + to_hi) * 2 + core, "tm": z * 2 + to_lo},
                device_id_type=MESH,
            ).start()
            return 0

        lax.fori_loop(1, 16, start, 0)

    p_start_at(z)

    def forward(s, _):
        slot = order(s)
        here = tiles.at[slot, mine]
        pltpu.make_async_copy(here, here, z_recv.at[slot]).wait()
        p_start_at(slot)
        return 0

    lax.fori_loop(1, 8, forward, 0)

    half = tiles.at[z, pl.ds(y_lo * 8, 8)]
    c_copy = pltpu.make_async_remote_copy(
        src_ref=half, dst_ref=other_half, send_sem=c_send, recv_sem=c_recv,
        device_id={"dof": partner, "tm": t}, device_id_type=MESH,
    )

    def accumulate(slot):
        both = tiles[slot]
        c = jnp.concatenate([both[:8].reshape(R, 128), both[8:].reshape(R, 128)], axis=1)
        hi = c.astype(jnp.bfloat16)
        rest = c - hi.astype(jnp.float32)
        mid = rest.astype(jnp.bfloat16)
        low = (rest - mid.astype(jnp.float32)).astype(jnp.bfloat16)
        table = jnp.concatenate([hi, mid, low, jnp.ones((R, 256), jnp.bfloat16)], axis=0)
        a = jnp.dot(hot_i[...], table, preferred_element_type=jnp.float32)
        b = jnp.dot(hot_j[...], table, preferred_element_type=jnp.float32)
        f = (a * b).astype(jnp.bfloat16)
        rows = f[:PAD]
        for n in range(2):
            gram_acc[n] += lax.dot_general(
                rows, f[(n + 1) * PAD : (n + 2) * PAD], (((1,), (1,)), ((), ())),
                preferred_element_type=jnp.float32,
            )

    wait_tiles(15, p_recv.at[z])
    c_copy.start()
    accumulate(z)

    def step(s, _):
        slot = order(s)
        wait_tiles(15, p_recv.at[slot])
        accumulate(slot)
        return 0

    lax.fori_loop(1, 8, step, 0)

    g_copy = pltpu.make_async_remote_copy(
        src_ref=gram_acc.at[1], dst_ref=gram_in, send_sem=g_send, recv_sem=g_recv,
        device_id={"dof": partner, "tm": t}, device_id_type=MESH,
    )
    g_copy.start()

    wait_tiles(15, rs_send)

    def z_done(k, _):
        z_copy(k).wait_send()
        return 0

    lax.fori_loop(1, 8, z_done, 0)

    def p_done(slot, _):
        wait_tiles(15, p_send.at[slot])
        return 0

    lax.fori_loop(0, 8, p_done, 0)
    c_copy.wait()
    own = tiles[z, pl.ds(y_lo * 8, 8)].reshape(R, 128)
    theirs = other_half[...].reshape(R, 128)
    coords_ref[:, :128] = jnp.where(core == 0, own, theirs)
    coords_ref[:, 128:] = jnp.where(core == 0, theirs, own)
    g_copy.wait()
    total = (gram_acc[0] + gram_in[...]) * (1.0 / NT)
    gram_ref[...] = total[:W, :W]


def on_device(snapshots, basis):
    rows, times = snapshots.shape
    vmem, dma = pltpu.VMEM, pltpu.SemaphoreType.DMA
    return pl.pallas_call(
        kernel,
        out_shape=(
            jax.ShapeDtypeStruct((W, W), jnp.float32),
            jax.ShapeDtypeStruct((R, times), jnp.float32),
        ),
        in_specs=[pl.BlockSpec(memory_space=pltpu.HBM)] * 2,
        out_specs=(pl.BlockSpec(memory_space=vmem), pl.BlockSpec(memory_space=vmem)),
        scratch_shapes=[
            vmem((R, rows), jnp.bfloat16),
            vmem((rows, times), jnp.bfloat16),
            vmem((3 * PAD, 256), jnp.bfloat16),
            vmem((3 * PAD, 256), jnp.bfloat16),
            vmem((16, 8, 128), jnp.float32),
            vmem((16, 8, 128), jnp.float32),
            vmem((8, 16, 8, 128), jnp.float32),
            vmem((2, PAD, PAD), jnp.float32),
            vmem((PAD, PAD), jnp.float32),
            vmem((8, 8, 128), jnp.float32),
            dma((2, CHUNKS)),
            dma, dma, dma((8,)), dma((8,)), dma((8,)), dma((8,)), dma, dma, dma, dma,
        ],
        compiler_params=pltpu.CompilerParams(
            collective_id=0, has_side_effects=True, vmem_limit_bytes=40 << 20
        ),
    )(basis.T, snapshots)


def solution(mesh):
    return jax.shard_map(
        on_device,
        mesh=mesh,
        in_specs=(P("dof", "tm"), P("dof", None)),
        out_specs=(P("tm", "dof"), P(None, "tm")),
        check_vma=False,
    )
```

time: 101 us -> 39.1 us (0.39)
  blocking collectives: 37.9 us -> 0 us
  Pallas kernels: 0 us -> 31.3 us
  local copies, waits for them, and re-layouts: 24 us -> 7 us
  waiting for transfers between devices: 17 us -> 0 us
  starting transfers between devices: 8.43 us -> 0 us
  matrix products: 6.3 us -> 0 us
  other arithmetic: 6.2 us -> 0 us
    all_to_all x1 -> x0, blocking collectives: 37.9 us -> none  [summed_on_arrival(): lax.all_to_all(parts, axis, split_axis=0, concat_axis=0, tiled=True)]
    pallas_call x0 -> x1, Pallas kernels: none -> 31.3 us  [on_device(): pl.pallas_call(kernel, out_shape=(jax.ShapeDtypeStruct((W, W), jnp.float3...]
    all_to_all x1 -> x0, waiting for transfers between devices: 17 us -> none  [sent_to_all(): return lax.all_to_all(copies, axis, split_axis=0, concat_axis=0, tiled=True)]
    gather x2 -> x0, local copies, waits for them, and re-layouts: 12.8 us -> none  [build_features(): quad = coords[upper_i, :] * coords[upper_j, :]]
    all_to_all x1 -> x0, starting transfers between devices: 8.43 us -> none  [sent_to_all(): return lax.all_to_all(copies, axis, split_axis=0, concat_axis=0, tiled=True)]
    dot_general x2 -> x0, matrix products: 6.3 us -> none  [the longest x1 5.79 us: on_device(): lax.dot_general(basis, snapshots, (((0,), (0,)), ((), ())), preferred_ele...]
    reshape x2 -> x0, local copies, waits for them, and re-layouts: 5.5 us -> none  [cut_along(): return jnp.moveaxis(shard.reshape(*before, size, -1, *after), dim, 0)]
    unnamed x8 -> x6, local copies, waits for them, and re-layouts: 1.76 us -> 7 us
  transfers between devices with their start and end apart: 1 -> 0, of which waited for: 1 -> 0; matrix products, arithmetic and copies ran while one was open for 0% -> 0% of each run, Pallas kernels for 0% -> 0%
where the time goes in v1:
time: 39.1 us; the launch traced here: 38.9 us
  Pallas kernels  31.3 us (80%)
  local copies, waits for them, and re-layouts  7 us (18%)
  between operations  0.65 us (2%)
    pallas_call x1, Pallas kernels, on_device(): pl.pallas_call(kernel, out_shape=(jax.ShapeDtypeStruct((W, W), jnp.float3...  31.3 us
    unnamed x6, local copies, waits for them, and re-layouts  7 us

profile of v1, /device:TPU:1, one launch (start us, length us, event | category | flops | bytes accessed | tf_op | source)
XLA Modules:
  0.0 38.9 jit_solution(7234010603979937701)
XLA Ops:
  0.6 0.0 copy-start
  0.6 4.0 %copy-done = bf16[20480,256]{1,0:T(8,128)(2,1)S(1)} copy-done((bf16[20480,256]{1,0:T(8,128)(2,1)S(1)}, bf16[20480,256]{1,0:T(8,128)(2,1)}, u32[]{:S(2)}) %copy-start) | copy-done | bytes 10485784
  4.6 0.0 copy-start.1
  4.6 1.7 %copy-done.1 = bf16[20480,64]{0,1:T(8,128)(2,1)S(1)} copy-done((bf16[20480,64]{0,1:T(8,128)(2,1)S(1)}, bf16[20480,64]{0,1:T(8,128)(2,1)}, u32[]{:S(2)}) %copy-start.1) | copy-done | bytes 2621464
  6.3 31.3 %shard_map.41 = (f32[134,134]{1,0:T(8,128)S(1)}, f32[64,256]{1,0:T(8,128)S(1)}) custom-call(bf16[64,20480]{1,0:T(8,128)(2,1)S(1)} %bitcast.1, bf16[20480,256]{1,0:T(8,128)(2,1)S(1)} %copy-done), custom_call_target="tpu_custom_call" | custom-call | tf_op jit(solution)/shard_map/pallas_call | solution.py:246
  37.6 0.7 %copy.6 = f32[134,134]{1,0:T(8,128)} copy(f32[134,134]{1,0:T(8,128)S(1)} %get-tuple-element.4) | data formatting | bytes 143648
  38.3 0.6 %copy.7 = f32[64,256]{1,0:T(8,128)} copy(f32[64,256]{1,0:T(8,128)S(1)} %get-tuple-element.5) | data formatting | bytes 131072
Async XLA Ops:
  0.6 4.0 %copy-start = (bf16[20480,256]{1,0:T(8,128)(2,1)S(1)}, bf16[20480,256]{1,0:T(8,128)(2,1)}, u32[]{:S(2)}) copy-start(bf16[20480,256]{1,0:T(8,128)(2,1)} %snap_hbm.1) | copy-start | bytes 31457284
  4.6 1.7 %copy-start.1 = (bf16[20480,64]{0,1:T(8,128)(2,1)S(1)}, bf16[20480,64]{0,1:T(8,128)(2,1)}, u32[]{:S(2)}) copy-start(bf16[20480,64]{0,1:T(8,128)(2,1)} %param.3) | copy-start | bytes 7864324
